TPU v7x, 256 devices: a whole 4x4x8 slice. The times are simulated.
256 devices in a mesh: table: 4 (over z_lo), row: 64 (over z_hi, y, x, core).
Axes of the slice: x: 4, y: 4, z: 8 (z_hi: 2, z_lo: 4; z = z_hi * 4 + z_lo), core: 2. Of those that a mesh axis runs over, the one named last changes fastest.
Arguments:
- tables: bfloat16 [4, 524288, 128], P('table', 'row'), may hold values from -3 to 3
- indices: int32 [4, 100, 512], P('table'), may hold values from 0 to 524287
- weights: bfloat16 [4, 100, 512], P('table'), may hold values from 0.19921875 to 1
- lengths: int32 [4, 512], P('table'), may hold values from 1 to 100, as said below
Outputs:
- pooled: bfloat16 [4, 512, 128], P(None, ('table', 'row'))
Inputs may be any that keep to these rules, and one draw needn't show every extreme that they name: `lengths`: the longest bag of each table has a power of two of at most 64 positions, or 100 positions, and some table has a bag of 100.
All inputs are finite; a program needn't handle non-finite values.
Results may differ from a plain program's by a relative error of at most 0.001.
Values may be sent and summed in bfloat16 or wider, within the bound.
No kernel may reach another device: no remote copies, remote signals or barrier semaphores. Data moves between devices by JAX's collectives and lax.ppermute only.
A program may use at most 64 MiB of HBM per device.

v0:
```python
import jax
import jax.numpy as jnp
from jax import lax
from jax.sharding import PartitionSpec as P

bag_block = 10


def cut_along(value, dim, peers):
    lengths = value.shape
    tiles = value.reshape(*lengths[:dim], peers, lengths[dim] // peers, *lengths[dim + 1 :])
    return jnp.moveaxis(tiles, dim, 0)


def sent_and_summed(value, axis, dim):
    tiles = cut_along(value, dim, lax.axis_size(axis))
    arrived = lax.all_to_all(tiles, axis, split_axis=0, concat_axis=0, tiled=True)
    return arrived.sum(axis=0)


def pool_local(table_rows, index_rows, weight, length, row_start, blocks):
    row_count = table_rows.shape[0]
    position = jnp.arange(index_rows.shape[0], dtype=jnp.int32)[:, None]
    local_index = index_rows - row_start
    inside = (local_index >= 0) & (local_index < row_count) & (position < length[None, :])
    factors = jnp.where(inside, weight, jnp.zeros_like(weight))
    local_index = jnp.clip(local_index, 0, row_count - 1)

    def add_block(block_number, running):
        first_row = block_number * bag_block
        index_block = lax.dynamic_slice_in_dim(local_index, first_row, bag_block, 0)
        factor_block = lax.dynamic_slice_in_dim(factors, first_row, bag_block, 0)
        gathered = jnp.take(table_rows, index_block, axis=0)
        return running + jnp.einsum(
            "lb,lbd->bd", factor_block, gathered, preferred_element_type=jnp.float32
        )

    empty = jnp.zeros((index_rows.shape[1], table_rows.shape[1]), jnp.float32)
    return lax.fori_loop(0, blocks, add_block, empty)


def on_device(tables, indices, weights, lengths):
    tab_dev, row_dev, feature_width = tables.shape
    batch_size = indices.shape[2]
    table_count = lax.axis_size("table")
    row_count = lax.axis_size("row")
    row_start = lax.axis_index("row") * row_dev
    blocks = indices.shape[1] // bag_block
    partial_list = [pool_local(tables[0], indices[0], weights[0], lengths[0], row_start, blocks)]
    partial_value = jnp.stack(partial_list, axis=0)
    grouped = partial_value.reshape(tab_dev, table_count, batch_size // table_count, feature_width)
    share_rows = batch_size // (table_count * row_count)
    shares = sent_and_summed(grouped, "row", 2)
    pooled = lax.all_to_all(
        shares.astype(jnp.bfloat16), "table", split_axis=1, concat_axis=0, tiled=True
    )
    return pooled.reshape(tab_dev * table_count, share_rows, feature_width)


def solution(mesh):
    placed = (
        P("table", "row", None),
        P("table", None, None),
        P("table", None, None),
        P("table", None),
    )
    return jax.shard_map(
        on_device,
        mesh=mesh,
        in_specs=placed,
        out_specs=P(None, ("table", "row"), None),
        check_vma=False,
    )
```

profile of v0, /device:TPU:1, one launch (start us, length us, event | category | flops | bytes accessed | tf_op | source)
XLA Modules:
  0.0 221.6 jit_solution(14330808285861031394)
XLA Ops:
  0.0 1.0 clamp_bitcast_fusion
  1.0 1.1 fusion.3
  2.0 180.5 %while.14 = (s32[]{:T(128)}, f32[512,128]{1,0:T(8,128)S(1)}, bf16[100,512]{1,0:T(8,128)(2,1)S(1)}, s32[100,512]{1,0:T(8,128)S(1)}, bf16[8192,128]{1,0:T(8,128)(2...) while((s32[]{:T(128)}, f32[512,128]{1,0:T(8,128)S(1)}, bf16[100,512]{1,0:T(8,128)(2,1)S(1)}, ...), condition=%wide.region_1.2_spmd.clone, body=%wide.region_0.1_spmd.clone.sunk | while | flops 2132999 | bytes 7807133 | solution.py:39
  2.1 15.6 %gather_fusion = bf16[5120,128]{1,0:T(8,128)(2,1)S(1)} fusion(bf16[8192,128]{1,0:T(8,128)(2,1)} %get-tuple-element.187, s32[5120]{0:T(1024)S(1)} %broadcast_clamp_fusion.2), kind=kCustom, calls=%fused_computation.clone.clone.1 | custom fusion | bytes 2641920 | tf_op jit(solution)/shard_map/while/body/eval_jaxpr/jit(_take)/gather | solution.py:33
  17.7 1.0 broadcast_select_fusion.2
  18.8 0.2 copy.22
  19.0 1.0 fusion.10
  20.2 15.6 %gather_fusion = bf16[5120,128]{1,0:T(8,128)(2,1)S(1)} fusion(bf16[8192,128]{1,0:T(8,128)(2,1)} %get-tuple-element.187, s32[5120]{0:T(1024)S(1)} %broadcast_clamp_fusion.2), kind=kCustom, calls=%fused_computation.clone.clone.1 | custom fusion | bytes 2641920 | tf_op jit(solution)/shard_map/while/body/eval_jaxpr/jit(_take)/gather | solution.py:33
  35.8 1.0 broadcast_select_fusion.2
  36.8 0.2 copy.22
  37.0 1.0 fusion.10
  38.2 15.6 %gather_fusion = bf16[5120,128]{1,0:T(8,128)(2,1)S(1)} fusion(bf16[8192,128]{1,0:T(8,128)(2,1)} %get-tuple-element.187, s32[5120]{0:T(1024)S(1)} %broadcast_clamp_fusion.2), kind=kCustom, calls=%fused_computation.clone.clone.1 | custom fusion | bytes 2641920 | tf_op jit(solution)/shard_map/while/body/eval_jaxpr/jit(_take)/gather | solution.py:33
  53.8 1.0 broadcast_select_fusion.2
  54.9 0.2 copy.22
  55.1 1.0 fusion.10
  56.3 15.6 %gather_fusion = bf16[5120,128]{1,0:T(8,128)(2,1)S(1)} fusion(bf16[8192,128]{1,0:T(8,128)(2,1)} %get-tuple-element.187, s32[5120]{0:T(1024)S(1)} %broadcast_clamp_fusion.2), kind=kCustom, calls=%fused_computation.clone.clone.1 | custom fusion | bytes 2641920 | tf_op jit(solution)/shard_map/while/body/eval_jaxpr/jit(_take)/gather | solution.py:33
  71.9 1.0 broadcast_select_fusion.2
  72.9 0.2 copy.22
  73.1 1.0 fusion.10
  74.3 15.6 %gather_fusion = bf16[5120,128]{1,0:T(8,128)(2,1)S(1)} fusion(bf16[8192,128]{1,0:T(8,128)(2,1)} %get-tuple-element.187, s32[5120]{0:T(1024)S(1)} %broadcast_clamp_fusion.2), kind=kCustom, calls=%fused_computation.clone.clone.1 | custom fusion | bytes 2641920 | tf_op jit(solution)/shard_map/while/body/eval_jaxpr/jit(_take)/gather | solution.py:33
  89.9 1.0 broadcast_select_fusion.2
  91.0 0.2 copy.22
  91.2 1.0 fusion.10
  92.4 15.6 %gather_fusion = bf16[5120,128]{1,0:T(8,128)(2,1)S(1)} fusion(bf16[8192,128]{1,0:T(8,128)(2,1)} %get-tuple-element.187, s32[5120]{0:T(1024)S(1)} %broadcast_clamp_fusion.2), kind=kCustom, calls=%fused_computation.clone.clone.1 | custom fusion | bytes 2641920 | tf_op jit(solution)/shard_map/while/body/eval_jaxpr/jit(_take)/gather | solution.py:33
  108.0 1.0 broadcast_select_fusion.2
  109.0 0.2 copy.22
  109.2 1.0 fusion.10
  110.4 15.6 %gather_fusion = bf16[5120,128]{1,0:T(8,128)(2,1)S(1)} fusion(bf16[8192,128]{1,0:T(8,128)(2,1)} %get-tuple-element.187, s32[5120]{0:T(1024)S(1)} %broadcast_clamp_fusion.2), kind=kCustom, calls=%fused_computation.clone.clone.1 | custom fusion | bytes 2641920 | tf_op jit(solution)/shard_map/while/body/eval_jaxpr/jit(_take)/gather | solution.py:33
  126.0 1.0 broadcast_select_fusion.2
  127.1 0.2 copy.22
  127.3 1.0 fusion.10
  128.5 15.6 %gather_fusion = bf16[5120,128]{1,0:T(8,128)(2,1)S(1)} fusion(bf16[8192,128]{1,0:T(8,128)(2,1)} %get-tuple-element.187, s32[5120]{0:T(1024)S(1)} %broadcast_clamp_fusion.2), kind=kCustom, calls=%fused_computation.clone.clone.1 | custom fusion | bytes 2641920 | tf_op jit(solution)/shard_map/while/body/eval_jaxpr/jit(_take)/gather | solution.py:33
  144.1 1.0 broadcast_select_fusion.2
  145.1 0.2 copy.22
  145.3 1.0 fusion.10
  146.5 15.6 %gather_fusion = bf16[5120,128]{1,0:T(8,128)(2,1)S(1)} fusion(bf16[8192,128]{1,0:T(8,128)(2,1)} %get-tuple-element.187, s32[5120]{0:T(1024)S(1)} %broadcast_clamp_fusion.2), kind=kCustom, calls=%fused_computation.clone.clone.1 | custom fusion | bytes 2641920 | tf_op jit(solution)/shard_map/while/body/eval_jaxpr/jit(_take)/gather | solution.py:33
  162.1 1.0 broadcast_select_fusion.2
  163.2 0.2 copy.22
  163.4 1.0 fusion.10
  164.6 15.6 %gather_fusion = bf16[5120,128]{1,0:T(8,128)(2,1)S(1)} fusion(bf16[8192,128]{1,0:T(8,128)(2,1)} %get-tuple-element.187, s32[5120]{0:T(1024)S(1)} %broadcast_clamp_fusion.2), kind=kCustom, calls=%fused_computation.clone.clone.1 | custom fusion | bytes 2641920 | tf_op jit(solution)/shard_map/while/body/eval_jaxpr/jit(_take)/gather | solution.py:33
  180.2 1.0 broadcast_select_fusion.2
  181.2 0.2 copy.22
  181.4 1.0 fusion.10
  182.6 0.1 copy.8
  182.7 28.8 %all_to_all.14 = f32[64,1,4,2,128]{4,3,2,1,0:T(2,128)S(1)} all-to-all(f32[64,1,4,2,128]{4,3,2,1,0:T(2,128)S(1)} %copy.8), channel_id=1, replica_groups=mesh['table'=4,'row'=64] {'row'}, dimensions={0} | all-to-all | bytes 524288 | tf_op jit(solution)/shard_map/all_to_all | solution.py:17
  211.4 0.1 reduce_sum.9
  211.5 9.5 %all_to_all.15 = bf16[1,4,2,128]{3,2,0,1:T(2,128)(2,1)S(1)} all-to-all(bf16[1,4,2,128]{3,2,0,1:T(2,128)(2,1)S(1)} %bitcast.33), channel_id=1, replica_groups=mesh['table'=4,'row'=64] {'table'}, dimensions={1} | all-to-all | bytes 4096 | tf_op jit(solution)/shard_map/all_to_all | solution.py:54
  221.0 0.6 copy.30
  (51 shorter events, 1.3 us)
where the time goes:
time: 222 us
  local copies, waits for them, and re-layouts  159 us (72%)
  blocking collectives  38.3 us (17%)
  other arithmetic  13.3 us (6%)
  matrix products  10.4 us (5%)
    gather x10, local copies, waits for them, and re-layouts, add_block(): gathered = jnp.take(table_rows, index_block, axis=0)  156 us
    all_to_all x1, blocking collectives, sent_and_summed(): lax.all_to_all(tiles, axis, split_axis=0, concat_axis=0, tiled=True)  28.8 us
    dot_general x10, matrix products, add_block(): jnp.einsum('lb,lbd->bd', factor_block, gathered, preferred_element_type=j...  10.4 us
    select_n x10, other arithmetic, add_block(): gathered = jnp.take(table_rows, index_block, axis=0)  10 us
    all_to_all x1, blocking collectives, on_device(): lax.all_to_all(shares.astype(jnp.bfloat16), 'table', split_axis=1, concat...  9.48 us

commit v1 on v0

v1 whole, which is shorter than its diff:
```python
import functools

import jax
import jax.numpy as jnp
from jax import lax
from jax.experimental import pallas as pl
from jax.experimental.pallas import tpu as pltpu
from jax.sharding import PartitionSpec as P

lanes = 128
packed_rows = 16
bags_per_step = 8
bags_per_dot = 256


def pool_kernel(
    start_ref,
    index_ref,
    weight_ref,
    length_ref,
    table_hbm,
    out_ref,
    table_ref,
    high_ref,
    low_ref,
    factor_ref,
    spread_ref,
    table_sem,
):
    table_copy = pltpu.make_async_copy(table_hbm, table_ref, table_sem)
    table_copy.start()
    bag, batch = index_ref.shape
    rows = table_ref.shape[0]
    tiles = rows // lanes
    stride = spread_ref.shape[0] // tiles

    local = index_ref[...] - start_ref[0]
    position = lax.broadcasted_iota(jnp.int32, (bag, batch), 0)
    inside = (local >= 0) & (local < rows) & (position < length_ref[...])
    local = jnp.where(inside, local, -1).astype(jnp.float32)
    weight = weight_ref[...].astype(jnp.float32)
    pad = lanes - bag
    local = jnp.concatenate([local, jnp.full((pad, batch), -1.0, jnp.float32)], 0)
    weight = jnp.concatenate([weight, jnp.zeros((pad, batch), jnp.float32)], 0)
    local = local.T.astype(jnp.int32)
    high_ref[...] = (local >> 7).astype(jnp.float32)
    low_ref[...] = (local & (lanes - 1)).astype(jnp.float32)
    factor_ref[...] = weight.T

    row_id = lax.broadcasted_iota(jnp.int32, (packed_rows, lanes), 0)
    row_ids = [
        (row_id + packed_rows * j).astype(jnp.float32).astype(jnp.bfloat16)
        for j in range(lanes // packed_rows)
    ]
    zero = jnp.zeros((packed_rows, lanes), jnp.bfloat16)
    one = jnp.ones((packed_rows, lanes), jnp.bfloat16)

    def row_of(ref, bag_number):
        row = ref[pl.ds(bag_number, 1), :]
        return jnp.broadcast_to(row, (packed_rows, lanes)).astype(jnp.bfloat16)

    def spread_bag(bag_number):
        high = row_of(high_ref, bag_number)
        low = row_of(low_ref, bag_number)
        factor = row_of(factor_ref, bag_number)
        by_high = [jnp.where(high == ids, factor, zero) for ids in row_ids[: tiles // packed_rows]]
        by_low = [jnp.where(low == ids, one, zero) for ids in row_ids]
        return lax.dot_general(
            jnp.concatenate(by_high, 0),
            jnp.concatenate(by_low, 0),
            (((1,), (1,)), ((), ())),
            preferred_element_type=jnp.float32,
        )

    def spread_step(step, carry):
        for k in range(bags_per_step):
            bag_number = step * bags_per_step + k
            spread_ref[pl.ds(bag_number, tiles, stride=stride), :] = spread_bag(bag_number)
        return carry

    lax.fori_loop(0, batch // bags_per_step, spread_step, 0)
    table_copy.wait()
    for first in range(0, batch, bags_per_dot):
        factors = jnp.concatenate(
            [spread_ref[pl.ds(j * stride + first, bags_per_dot), :] for j in range(tiles)], 1
        )
        upper = factors.astype(jnp.bfloat16)
        rest = (factors - upper.astype(jnp.float32)).astype(jnp.bfloat16)
        table = table_ref[...]
        total = jnp.dot(upper, table, preferred_element_type=jnp.float32)
        total = total + jnp.dot(rest, table, preferred_element_type=jnp.float32)
        out_ref[pl.ds(first, bags_per_dot), :] = total


def pool_local(table_rows, index_rows, weight, length, row_start):
    rows, width = table_rows.shape
    batch = index_rows.shape[1]
    vmem = pl.BlockSpec(memory_space=pltpu.VMEM)
    return pl.pallas_call(
        pool_kernel,
        out_shape=jax.ShapeDtypeStruct((batch, width), jnp.float32),
        in_specs=[
            pl.BlockSpec(memory_space=pltpu.SMEM),
            vmem,
            vmem,
            vmem,
            pl.BlockSpec(memory_space=pl.ANY),
        ],
        out_specs=vmem,
        scratch_shapes=[
            pltpu.VMEM((rows, width), table_rows.dtype),
            pltpu.VMEM((batch, lanes), jnp.float32),
            pltpu.VMEM((batch, lanes), jnp.float32),
            pltpu.VMEM((batch, lanes), jnp.float32),
            pltpu.VMEM(((batch + 1) * (rows // lanes), lanes), jnp.float32),
            pltpu.SemaphoreType.DMA,
        ],
    )(row_start.reshape(1), index_rows, weight, length, table_rows)


def on_device(tables, indices, weights, lengths):
    _, row_dev, feature_width = tables.shape
    batch_size = indices.shape[2]
    table_count = lax.axis_size("table")
    row_count = lax.axis_size("row")
    row_start = (lax.axis_index("row") * row_dev).astype(jnp.int32)
    partial = pool_local(tables[0], indices[0], weights[0], lengths, row_start)
    share = batch_size // (table_count * row_count)
    tiles = partial.reshape(table_count * row_count, share, feature_width)
    arrived = lax.all_to_all(tiles, ("table", "row"), split_axis=0, concat_axis=0, tiled=True)
    shares = arrived.reshape(table_count, row_count, share, feature_width)
    return shares.sum(axis=1).astype(jnp.bfloat16)


def solution(mesh):
    placed = (
        P("table", "row", None),
        P("table", None, None),
        P("table", None, None),
        P("table", None),
    )
    return jax.shard_map(
        on_device,
        mesh=mesh,
        in_specs=placed,
        out_specs=P(None, ("table", "row"), None),
        check_vma=False,
    )
```

time: 222 us -> 58.3 us (0.26)
  local copies, waits for them, and re-layouts: 159 us -> 1.63 us
  Pallas kernels: 0 us -> 24.3 us
  other arithmetic: 13.3 us -> 0.65 us
  matrix products: 10.4 us -> 0 us
  blocking collectives: 38.3 us -> 31.5 us
    gather x10 -> x0, local copies, waits for them, and re-layouts: 156 us -> none  [add_block(): gathered = jnp.take(table_rows, index_block, axis=0)]
    pallas_call x0 -> x1, Pallas kernels: none -> 24.3 us  [pool_local(): pl.pallas_call(pool_kernel, out_shape=jax.ShapeDtypeStruct((batch, width)...]
    select_n x11 -> x0, other arithmetic: 11.1 us -> none  [the longest x10 10 us: add_block(): gathered = jnp.take(table_rows, index_block, axis=0)]
    dot_general x10 -> x0, matrix products: 10.4 us -> none  [add_block(): jnp.einsum('lb,lbd->bd', factor_block, gathered, preferred_element_type=j...]
    all_to_all x2 -> x1, blocking collectives: 38.3 us -> 31.5 us  [on_device(): lax.all_to_all(tiles, ('table', 'row'), split_axis=0, concat_axis=0, tile...]
where the time goes in v1:
time: 58.3 us; the launch traced here: 58.1 us
  blocking collectives  31.5 us (54%)
  Pallas kernels  24.3 us (42%)
  local copies, waits for them, and re-layouts  1.63 us (3%)
  other arithmetic  0.65 us (1%)
    all_to_all x1, blocking collectives, on_device(): lax.all_to_all(tiles, ('table', 'row'), split_axis=0, concat_axis=0, tile...  31.5 us
    pallas_call x1, Pallas kernels, pool_local(): pl.pallas_call(pool_kernel, out_shape=jax.ShapeDtypeStruct((batch, width)...  24.3 us
    unnamed x1, local copies, waits for them, and re-layouts  1.63 us

profile of v1, /device:TPU:1, one launch (start us, length us, event | category | flops | bytes accessed | tf_op | source)
XLA Modules:
  0.0 58.1 jit_solution(1850451695283951316)
XLA Ops:
  0.0 1.6 %copy.7 = s32[1,100,512]{2,1,0:T(8,128)} copy(s32[1,100,512]{2,0,1:T(1,128)} %param.5) | data formatting | bytes 409600
  1.6 24.3 %shard_map.46 = f32[512,128]{1,0:T(8,128)} custom-call(s32[1]{0:T(128)} %bitcast.start_ref, s32[100,512]{1,0:T(8,128)} %bitcast.11, bf16[100,512]{1,0:T(8,128)(2,1)} %bitcast.12, s32[1,512]{1,0:T(1,128)} %length_ref.1, bf16[8192,128]{1,0:T(8,128)(2,1)} %bitcast.9), custom_call_target="tpu_custom_call" | custom-call | tf_op jit(solution)/shard_map/pallas_call | solution.py:99
  25.9 31.5 %all_to_all.5 = f32[256,2,128]{2,1,0:T(2,128)S(1)} all-to-all(f32[256,2,128]{2,1,0:T(2,128)} %bitcast.10), channel_id=1, replica_groups=mesh['table'=4,'row'=64] {'table','row'}, dimensions={0} | all-to-all | bytes 524288 | tf_op jit(solution)/shard_map/all_to_all | solution.py:130
  57.5 0.7 %bitcast_reduce_fusion = bf16[4,2,128]{2,1,0:T(2,128)(2,1)} fusion(f32[256,2,128]{2,1,0:T(2,128)S(1)} %all_to_all.5), kind=kLoop, calls=%fused_computation | loop fusion | flops 64512 | bytes 264192 | tf_op jit(solution)/shard_map/reduce_sum | solution.py:132

commit v2 on v1

v2 whole, which is shorter than its diff:
```python
import jax
import jax.numpy as jnp
from jax import lax
from jax.experimental import pallas as pl
from jax.experimental.pallas import tpu as pltpu
from jax.sharding import PartitionSpec as P

lanes = 128
packed_rows = 16
slots = 16
weight_unit = 1024
groups_per_step = 4
bags_per_dot = 256


def pool_kernel(
    start_ref,
    index_ref,
    weight_ref,
    length_ref,
    table_hbm,
    out_ref,
    table_ref,
    rank_ref,
    code_ref,
    high_ref,
    low_ref,
    factor_ref,
    spread_ref,
    table_sem,
):
    table_copy = pltpu.make_async_copy(table_hbm, table_ref, table_sem)
    table_copy.start()
    bag, _, batch = index_ref.shape
    rows = table_ref.shape[0]
    tiles = rows // lanes
    octets = tiles // 8
    stride = spread_ref.shape[0] // tiles
    blocks = batch // lanes
    padded = rank_ref.shape[0]
    groups = high_ref.shape[0]
    group_bags = lanes // slots

    local = index_ref[:, 0, :] - start_ref[0]
    position = lax.broadcasted_iota(jnp.int32, (bag, batch), 0)
    inside = (local >= 0) & (local < rows) & (position < length_ref[...])
    code = local.astype(jnp.float32) * (2.0 * weight_unit)
    code = code + weight_ref[...].astype(jnp.float32) * weight_unit
    code_ref[:bag, :] = jnp.where(inside, code, 0.0)
    code_ref[bag:, :] = jnp.zeros((padded - bag, batch), jnp.float32)

    used = jnp.where(inside, 1.0, 0.0)
    used = jnp.concatenate([used, jnp.zeros((lanes - bag, batch), jnp.float32)], 0)
    before = lax.broadcasted_iota(jnp.int32, (padded, lanes), 0) > lax.broadcasted_iota(
        jnp.int32, (padded, lanes), 1
    )
    rank = jnp.dot(
        jnp.where(before, 1.0, 0.0).astype(jnp.bfloat16),
        used.astype(jnp.bfloat16),
        preferred_element_type=jnp.float32,
    )
    rank_ref[...] = rank
    rounds = (jnp.max(rank[padded - 1 :, :]).astype(jnp.int32) + (slots - 1)) // slots

    row_id = lax.broadcasted_iota(jnp.int32, (packed_rows, lanes), 0)
    row_ids = [
        (row_id + packed_rows * i).astype(jnp.float32).astype(jnp.bfloat16)
        for i in range(lanes // packed_rows)
    ]
    zero = jnp.zeros((packed_rows, lanes), jnp.bfloat16)
    one = jnp.ones((packed_rows, lanes), jnp.bfloat16)
    owner = lax.broadcasted_iota(jnp.int32, (packed_rows, lanes), 1) // slots
    owner = owner.astype(jnp.float32).astype(jnp.bfloat16)
    owned = [owner == jnp.full_like(owner, g) for g in range(group_bags)]

    def fill_slots(first):
        planes = []
        for block in range(blocks):
            where = pl.ds(block * lanes, lanes)
            rank = rank_ref[:, where]
            code = code_ref[:, where]
            for s in range(slots):
                at = rank == (first + s).astype(jnp.float32)
                planes.append(jnp.sum(jnp.where(at, code, 0.0), axis=0, keepdims=True))
        plane = jnp.concatenate(planes, 0)
        plane = jnp.concatenate([plane, pltpu.roll(plane, lanes - groups, 1)], 0)
        code = plane.T[:groups].astype(jnp.int32)
        row = code // (2 * weight_unit)
        high_ref[...] = (row // lanes).astype(jnp.float32)
        low_ref[...] = (row % lanes).astype(jnp.float32)
        factor = (code % (2 * weight_unit)).astype(jnp.float32)
        factor_ref[...] = factor * (1.0 / weight_unit)

    def row_of(ref, j):
        row = ref[pl.ds(j, 1), :]
        return jnp.broadcast_to(row, (packed_rows, lanes)).astype(jnp.bfloat16)

    def spread_group(j):
        high = row_of(high_ref, j)
        low = row_of(low_ref, j)
        factor = row_of(factor_ref, j)
        at = [high == ids for ids in row_ids[: tiles // packed_rows]]
        by_high = []
        for g in range(group_bags):
            mine = jnp.where(owned[g], factor, zero)
            by_high += [jnp.where(hit, mine, zero) for hit in at]
        by_low = [jnp.where(low == ids, one, zero) for ids in row_ids]
        return lax.dot_general(
            jnp.concatenate(by_high, 0),
            jnp.concatenate(by_low, 0),
            (((1,), (1,)), ((), ())),
            preferred_element_type=jnp.float32,
        )

    def spread_step(step, inexact, add):
        inexact = list(inexact)
        for k in range(groups_per_step):
            j = step * groups_per_step + k
            total = spread_group(j)
            for g in range(group_bags):
                first = (g % blocks) * lanes + (g // blocks) * groups
                where = pl.ds(first + j, tiles, stride=stride)
                part = total[g * tiles : (g + 1) * tiles]
                if add:
                    part = part + spread_ref[where, :]
                spread_ref[where, :] = part
                rest = jnp.abs(part - part.astype(jnp.bfloat16).astype(jnp.float32))
                for o in range(octets):
                    inexact[o] = jnp.maximum(inexact[o], rest[o * 8 : (o + 1) * 8])
        return tuple(inexact)

    def spread_round(inexact, add):
        return lax.fori_loop(
            0,
            groups // groups_per_step,
            lambda step, found: spread_step(step, found, add),
            inexact,
        )

    def later_round(number, inexact):
        fill_slots(number * slots)
        return spread_round(inexact, True)

    fill_slots(jnp.int32(0))
    inexact = tuple(jnp.zeros((8, lanes), jnp.float32) for _ in range(octets))
    inexact = spread_round(inexact, False)
    inexact = lax.fori_loop(1, rounds, later_round, inexact)

    table_copy.wait()
    for first in range(0, batch, bags_per_dot):
        factors = [
            spread_ref[pl.ds(i * stride + first, bags_per_dot), :].astype(jnp.bfloat16)
            for i in range(tiles)
        ]
        out_ref[pl.ds(first, bags_per_dot), :] = jnp.dot(
            jnp.concatenate(factors, 1), table_ref[...], preferred_element_type=jnp.float32
        )

    for o in range(octets):

        @pl.when(jnp.max(inexact[o]) > 0)
        def _(o=o):
            factors = jnp.concatenate(
                [spread_ref[pl.ds((8 * o + i) * stride, batch), :] for i in range(8)], 1
            )
            rest = factors - factors.astype(jnp.bfloat16).astype(jnp.float32)
            out_ref[...] += jnp.dot(
                rest.astype(jnp.bfloat16),
                table_ref[pl.ds(8 * o * lanes, 8 * lanes), :],
                preferred_element_type=jnp.float32,
            )


def pool_local(table_rows, index_rows, weight, length, row_start):
    rows, width = table_rows.shape
    bag, batch = weight.shape
    padded = bag + 8 - bag % 8
    groups = batch * slots // lanes
    vmem = pl.BlockSpec(memory_space=pltpu.VMEM)
    by_position = pltpu.VMEM((padded, batch), jnp.float32)
    by_group = pltpu.VMEM((groups, lanes), jnp.float32)
    return pl.pallas_call(
        pool_kernel,
        out_shape=jax.ShapeDtypeStruct((batch, width), jnp.float32),
        in_specs=[
            pl.BlockSpec(memory_space=pltpu.SMEM),
            vmem,
            vmem,
            vmem,
            pl.BlockSpec(memory_space=pl.ANY),
        ],
        out_specs=vmem,
        scratch_shapes=[
            pltpu.VMEM((rows, width), table_rows.dtype),
            by_position,
            by_position,
            by_group,
            by_group,
            by_group,
            pltpu.VMEM(((batch + 1) * (rows // lanes), lanes), jnp.float32),
            pltpu.SemaphoreType.DMA,
        ],
    )(row_start.reshape(1), index_rows, weight, length, table_rows)


def on_device(tables, indices, weights, lengths):
    _, row_dev, feature_width = tables.shape
    batch_size = indices.shape[2]
    table_count = lax.axis_size("table")
    row_count = lax.axis_size("row")
    row_start = (lax.axis_index("row") * row_dev).astype(jnp.int32)
    index_rows = indices.transpose(1, 0, 2)
    partial = pool_local(tables[0], index_rows, weights[0], lengths, row_start)
    share = batch_size // (table_count * row_count)
    tiles = partial.reshape(table_count * row_count, share, feature_width)
    arrived = lax.all_to_all(tiles, ("table", "row"), split_axis=0, concat_axis=0, tiled=True)
    shares = arrived.reshape(table_count, row_count, share, feature_width)
    return shares.sum(axis=1).astype(jnp.bfloat16)


def solution(mesh):
    placed = (
        P("table", "row", None),
        P("table", None, None),
        P("table", None, None),
        P("table", None),
    )
    return jax.shard_map(
        on_device,
        mesh=mesh,
        in_specs=placed,
        out_specs=P(None, ("table", "row"), None),
        check_vma=False,
    )
```

time: 58.3 us -> 43.6 us (0.75)
  Pallas kernels: 24.3 us -> 11.5 us
  local copies, waits for them, and re-layouts: 1.63 us -> 0 us
    pallas_call x1, Pallas kernels: 24.3 us -> 11.5 us  [pool_local(): pl.pallas_call(pool_kernel, out_shape=jax.ShapeDtypeStruct((batch, width)...]
    unnamed x1 -> x0, local copies, waits for them, and re-layouts: 1.63 us -> none
where the time goes in v2:
time: 43.6 us; the launch traced here: 43.2 us
  blocking collectives  31.1 us (71%)
  Pallas kernels  11.5 us (26%)
  other arithmetic  0.65 us (1%)
    all_to_all x1, blocking collectives, on_device(): lax.all_to_all(tiles, ('table', 'row'), split_axis=0, concat_axis=0, tile...  31.1 us
    pallas_call x1, Pallas kernels, pool_local(): pl.pallas_call(pool_kernel, out_shape=jax.ShapeDtypeStruct((batch, width)...  11.5 us

profile of v2, /device:TPU:1, one launch (start us, length us, event | category | flops | bytes accessed | tf_op | source)
XLA Modules:
  0.0 43.2 jit_solution(7138558469483574525)
XLA Ops:
  0.0 11.5 %shard_map.46 = f32[512,128]{1,0:T(8,128)} custom-call(s32[1]{0:T(128)} %bitcast.start_ref, s32[100,1,512]{2,1,0:T(1,128)} %bitcast.9, bf16[100,512]{1,0:T(8,128)(2,1)} %bitcast.10, s32[1,512]{1,0:T(1,128)} %length_ref.1, bf16[8192,128]{1,0:T(8,128)(2,1)} %bitcast.7), custom_call_target="tpu_custom_call" | custom-call | tf_op jit(solution)/shard_map/pallas_call | solution.py:182
  11.5 31.1 %all_to_all.5 = f32[256,2,128]{2,1,0:T(2,128)S(1)} all-to-all(f32[256,2,128]{2,1,0:T(2,128)} %bitcast.8), channel_id=1, replica_groups=mesh['table'=4,'row'=64] {'table','row'}, dimensions={0} | all-to-all | bytes 524288 | tf_op jit(solution)/shard_map/all_to_all | solution.py:216
  42.5 0.7 %bitcast_reduce_fusion = bf16[4,2,128]{2,1,0:T(2,128)(2,1)} fusion(f32[256,2,128]{2,1,0:T(2,128)S(1)} %all_to_all.5), kind=kLoop, calls=%fused_computation | loop fusion | flops 64512 | bytes 264192 | tf_op jit(solution)/shard_map/reduce_sum | solution.py:218

commit v3 on v2

--- a/solution.py
+++ b/solution.py
@@ -9,7 +9,8 @@
 packed_rows = 16
 slots = 16
 weight_unit = 1024
-groups_per_step = 4
+groups_per_step = 32
+vmem_bytes = 24 * 2**20
 bags_per_dot = 256
 
 
@@ -187,7 +188,7 @@
             vmem,
             vmem,
             vmem,
-            pl.BlockSpec(memory_space=pl.ANY),
+            pl.BlockSpec(memory_space=pltpu.HBM),
         ],
         out_specs=vmem,
         scratch_shapes=[
@@ -200,6 +201,7 @@
             pltpu.VMEM(((batch + 1) * (rows // lanes), lanes), jnp.float32),
             pltpu.SemaphoreType.DMA,
         ],
+        compiler_params=pltpu.CompilerParams(vmem_limit_bytes=vmem_bytes),
     )(row_start.reshape(1), index_rows, weight, length, table_rows)
 
 

time: 43.6 us -> 44.1 us (1.011); the launches traced: 43.2 us -> 44.2 us
  local copies, waits for them, and re-layouts: 0 us -> 4.1 us
  Pallas kernels: 11.5 us -> 7.64 us
  blocking collectives: 31.1 us -> 31.8 us
    unnamed x0 -> x8, local copies, waits for them, and re-layouts: none -> 4.1 us
    pallas_call x1, Pallas kernels: 11.5 us -> 7.64 us  [pool_local(): pl.pallas_call(pool_kernel, out_shape=jax.ShapeDtypeStruct((batch, width)...]
    all_to_all x1, blocking collectives: 31.1 us -> 31.8 us  [on_device(): lax.all_to_all(tiles, ('table', 'row'), split_axis=0, concat_axis=0, tile...]
where the time goes in v3:
time: 44.1 us; the launch traced here: 44.2 us
  blocking collectives  31.8 us (72%)
  Pallas kernels  7.64 us (17%)
  local copies, waits for them, and re-layouts  4.1 us (9%)
  other arithmetic  0.65 us (1%)
    all_to_all x1, blocking collectives, on_device(): lax.all_to_all(tiles, ('table', 'row'), split_axis=0, concat_axis=0, tile...  31.8 us
    pallas_call x1, Pallas kernels, pool_local(): pl.pallas_call(pool_kernel, out_shape=jax.ShapeDtypeStruct((batch, width)...  7.64 us
    unnamed x8, local copies, waits for them, and re-layouts  4.1 us

profile of v3, /device:TPU:1, one launch (start us, length us, event | category | flops | bytes accessed | tf_op | source)
XLA Modules:
  0.0 44.2 jit_solution(17914158409119421549)
XLA Ops:
  0.0 0.0 copy-start
  0.0 1.6 %copy-done = bf16[1,8192,128]{2,1,0:T(8,128)(2,1)S(1)} copy-done((bf16[1,8192,128]{2,1,0:T(8,128)(2,1)S(1)}, bf16[1,8192,128]{2,1,0:T(8,128)(2,1)}, u32[]{:S(2)}) %copy-start) | copy-done | bytes 2097176
  1.6 0.0 copy-start.1
  1.6 0.9 %copy-done.1 = s32[1,100,512]{2,0,1:T(1,128)S(1)} copy-done((s32[1,100,512]{2,0,1:T(1,128)S(1)}, s32[1,100,512]{2,0,1:T(1,128)}, u32[]{:S(2)}) %copy-start.1) | copy-done | bytes 204824
  2.5 0.0 copy-start.2
  2.5 0.9 %copy-done.2 = bf16[1,100,512]{2,1,0:T(8,128)(2,1)S(1)} copy-done((bf16[1,100,512]{2,1,0:T(8,128)(2,1)S(1)}, bf16[1,100,512]{2,1,0:T(8,128)(2,1)}, u32[]{:S(2)}) %copy-start.2) | copy-done | bytes 102424
  3.4 0.0 copy-start.3
  3.4 0.7 %copy-done.3 = s32[1,512]{1,0:T(1,128)S(1)} copy-done((s32[1,512]{1,0:T(1,128)S(1)}, s32[1,512]{1,0:T(1,128)}, u32[]{:S(2)}) %copy-start.3) | copy-done | bytes 2072
  4.1 7.6 %shard_map.46 = f32[512,128]{1,0:T(8,128)S(1)} custom-call(s32[1]{0:T(128)} %bitcast.start_ref, s32[100,1,512]{2,1,0:T(1,128)S(1)} %bitcast.9, bf16[100,512]{1,0:T(8,128)(2,1)S(1)} %bitcast.10, s32[1,512]{1,0:T(1,128)S(1)} %copy-done.3, bf16[8192,128]{1,0:T(8,128)(2,1)S(1)} %bitcast.7), custom_call_target="tpu_custom_call" | custom-call | tf_op jit(solution)/shard_map/pallas_call | solution.py:183
  11.7 31.8 %all_to_all.5 = f32[256,2,128]{2,1,0:T(2,128)S(1)} all-to-all(f32[256,2,128]{2,1,0:T(2,128)S(1)} %bitcast.8), channel_id=1, replica_groups=mesh['table'=4,'row'=64] {'table','row'}, dimensions={0} | all-to-all | bytes 524288 | tf_op jit(solution)/shard_map/all_to_all | solution.py:218
  43.5 0.7 %bitcast_reduce_fusion = bf16[4,2,128]{2,1,0:T(2,128)(2,1)} fusion(f32[256,2,128]{2,1,0:T(2,128)S(1)} %all_to_all.5), kind=kLoop, calls=%fused_computation | loop fusion | flops 64512 | bytes 264192 | tf_op jit(solution)/shard_map/reduce_sum | solution.py:220
Async XLA Ops:
  0.0 1.6 %copy-start = (bf16[1,8192,128]{2,1,0:T(8,128)(2,1)S(1)}, bf16[1,8192,128]{2,1,0:T(8,128)(2,1)}, u32[]{:S(2)}) copy-start(bf16[1,8192,128]{2,1,0:T(8,128)(2,1)} %param.4) | copy-start | bytes 6291460
  1.6 0.9 %copy-start.1 = (s32[1,100,512]{2,0,1:T(1,128)S(1)}, s32[1,100,512]{2,0,1:T(1,128)}, u32[]{:S(2)}) copy-start(s32[1,100,512]{2,0,1:T(1,128)} %param.5) | copy-start | bytes 614404
  2.5 0.9 %copy-start.2 = (bf16[1,100,512]{2,1,0:T(8,128)(2,1)S(1)}, bf16[1,100,512]{2,1,0:T(8,128)(2,1)}, u32[]{:S(2)}) copy-start(bf16[1,100,512]{2,1,0:T(8,128)(2,1)} %param.6) | copy-start | bytes 307204
  3.4 0.7 %copy-start.3 = (s32[1,512]{1,0:T(1,128)S(1)}, s32[1,512]{1,0:T(1,128)}, u32[]{:S(2)}) copy-start(s32[1,512]{1,0:T(1,128)} %length_ref.1) | copy-start | bytes 6148

commit v4 on v2

--- a/solution.py
+++ b/solution.py
@@ -9,7 +9,7 @@
 packed_rows = 16
 slots = 16
 weight_unit = 1024
-groups_per_step = 4
+groups_per_step = 32
 bags_per_dot = 256
 
 

time: 43.6 us -> 42.3 us (0.970); the launches traced: 43.2 us -> 42.5 us
  Pallas kernels: 11.5 us -> 10.5 us
    pallas_call x1, Pallas kernels: 11.5 us -> 10.5 us  [pool_local(): pl.pallas_call(pool_kernel, out_shape=jax.ShapeDtypeStruct((batch, width)...]
where the time goes in v4:
time: 42.3 us; the launch traced here: 42.5 us
  blocking collectives  31.3 us (74%)
  Pallas kernels  10.5 us (25%)
  other arithmetic  0.65 us (2%)
    all_to_all x1, blocking collectives, on_device(): lax.all_to_all(tiles, ('table', 'row'), split_axis=0, concat_axis=0, tile...  31.3 us
    pallas_call x1, Pallas kernels, pool_local(): pl.pallas_call(pool_kernel, out_shape=jax.ShapeDtypeStruct((batch, width)...  10.5 us

profile of v4, /device:TPU:1, one launch (start us, length us, event | category | flops | bytes accessed | tf_op | source)
XLA Modules:
  0.0 42.5 jit_solution(8496305389996660090)
XLA Ops:
  0.0 10.5 %shard_map.46 = f32[512,128]{1,0:T(8,128)} custom-call(s32[1]{0:T(128)} %bitcast.start_ref, s32[100,1,512]{2,1,0:T(1,128)} %bitcast.9, bf16[100,512]{1,0:T(8,128)(2,1)} %bitcast.10, s32[1,512]{1,0:T(1,128)} %length_ref.1, bf16[8192,128]{1,0:T(8,128)(2,1)} %bitcast.7), custom_call_target="tpu_custom_call" | custom-call | tf_op jit(solution)/shard_map/pallas_call | solution.py:182
  10.5 31.3 %all_to_all.5 = f32[256,2,128]{2,1,0:T(2,128)S(1)} all-to-all(f32[256,2,128]{2,1,0:T(2,128)} %bitcast.8), channel_id=1, replica_groups=mesh['table'=4,'row'=64] {'table','row'}, dimensions={0} | all-to-all | bytes 524288 | tf_op jit(solution)/shard_map/all_to_all | solution.py:216
  41.9 0.7 %bitcast_reduce_fusion = bf16[4,2,128]{2,1,0:T(2,128)(2,1)} fusion(f32[256,2,128]{2,1,0:T(2,128)S(1)} %all_to_all.5), kind=kLoop, calls=%fused_computation | loop fusion | flops 64512 | bytes 264192 | tf_op jit(solution)/shard_map/reduce_sum | solution.py:218

commit v5 on v0

v5 whole, which is shorter than its diff:
```python
import jax
import jax.numpy as jnp
from jax import lax
from jax.experimental import pallas as pl
from jax.experimental.pallas import tpu as pltpu
from jax.sharding import Mesh
from jax.sharding import PartitionSpec as P

lanes = 128
packed_rows = 16
slots = 16
weight_unit = 1024


def read_positions(start_ref, index_ref, weight_ref, length_ref, rank_ref, code_ref, rows):
    bag, _, batch = index_ref.shape
    padded = rank_ref.shape[0]
    local = index_ref[:, 0, :] - start_ref[0]
    position = lax.broadcasted_iota(jnp.int32, (bag, batch), 0)
    inside = (local >= 0) & (local < rows) & (position < length_ref[...])
    code = local.astype(jnp.float32) * (2.0 * weight_unit)
    code = code + weight_ref[...].astype(jnp.float32) * weight_unit
    code_ref[:bag, :] = jnp.where(inside, code, 0.0)
    code_ref[bag:, :] = jnp.zeros((padded - bag, batch), jnp.float32)

    used = jnp.where(inside, 1.0, 0.0)
    used = jnp.concatenate([used, jnp.zeros((lanes - bag, batch), jnp.float32)], 0)
    before = lax.broadcasted_iota(jnp.int32, (padded, lanes), 0) > lax.broadcasted_iota(
        jnp.int32, (padded, lanes), 1
    )
    rank = jnp.dot(
        jnp.where(before, 1.0, 0.0).astype(jnp.bfloat16),
        used.astype(jnp.bfloat16),
        preferred_element_type=jnp.float32,
    )
    rank_ref[...] = rank
    return (jnp.max(rank[padded - 1 :, :]).astype(jnp.int32) + (slots - 1)) // slots


def fill_slots(rank_ref, code_ref, slot_refs, first):
    high_ref, low_ref, factor_ref = slot_refs
    groups = high_ref.shape[0]
    planes = []
    for block in range(rank_ref.shape[1] // lanes):
        where = pl.ds(block * lanes, lanes)
        rank = rank_ref[:, where]
        code = code_ref[:, where]
        for s in range(slots):
            at = rank == (first + s).astype(jnp.float32)
            planes.append(jnp.sum(jnp.where(at, code, 0.0), axis=0, keepdims=True))
    plane = jnp.concatenate(planes, 0)
    plane = jnp.concatenate([plane, pltpu.roll(plane, lanes - groups, 1)], 0)
    code = plane.T[:groups].astype(jnp.int32)
    row = code // (2 * weight_unit)
    high_ref[...] = (row // lanes).astype(jnp.float32)
    low_ref[...] = (row % lanes).astype(jnp.float32)
    factor = (code % (2 * weight_unit)).astype(jnp.float32)
    factor_ref[...] = factor * (1.0 / weight_unit)


def spread_half(slot_refs, spread_ref, core, tiles, inexact, add):
    high_ref, low_ref, factor_ref = slot_refs
    group_bags = lanes // slots
    half_groups = high_ref.shape[0] // 2
    stride = spread_ref.shape[0] // tiles
    row_id = lax.broadcasted_iota(jnp.int32, (packed_rows, lanes), 0)
    row_ids = [
        (row_id + packed_rows * i).astype(jnp.float32).astype(jnp.bfloat16)
        for i in range(lanes // packed_rows)
    ]
    zero = jnp.zeros((packed_rows, lanes), jnp.bfloat16)
    one = jnp.ones((packed_rows, lanes), jnp.bfloat16)
    owner = lax.broadcasted_iota(jnp.int32, (packed_rows, lanes), 1) // slots
    owner = owner.astype(jnp.float32).astype(jnp.bfloat16)
    owned = [owner == jnp.full_like(owner, g) for g in range(group_bags)]
    inexact = list(inexact)

    def row_of(ref, j):
        row = ref[pl.ds(j, 1), :]
        return jnp.broadcast_to(row, (packed_rows, lanes)).astype(jnp.bfloat16)

    for t in range(half_groups):
        j = t // 2 * 4 + t % 2 + 2 * core
        high = row_of(high_ref, j)
        low = row_of(low_ref, j)
        factor = row_of(factor_ref, j)
        at = [high == ids for ids in row_ids[: tiles // packed_rows]]
        by_high = []
        for g in range(group_bags):
            mine = jnp.where(owned[g], factor, zero)
            by_high += [jnp.where(hit, mine, zero) for hit in at]
        by_low = [jnp.where(low == ids, one, zero) for ids in row_ids]
        total = lax.dot_general(
            jnp.concatenate(by_high, 0),
            jnp.concatenate(by_low, 0),
            (((1,), (1,)), ((), ())),
            preferred_element_type=jnp.float32,
        )
        blocks = group_bags // 2
        for g in range(group_bags):
            first = (g % blocks * 2 + g // blocks) * half_groups
            where = pl.ds(first + t, tiles, stride=stride)
            part = total[g * tiles : (g + 1) * tiles]
            if add:
                part = part + spread_ref[where, :]
            spread_ref[where, :] = part
            rest = jnp.abs(part - part.astype(jnp.bfloat16).astype(jnp.float32))
            for o in range(len(inexact)):
                inexact[o] = jnp.maximum(inexact[o], rest[o * 8 : (o + 1) * 8])
    return tuple(inexact)


def multiply(spread_ref, table_ref, inexact, out_ref):
    tiles = table_ref.shape[0] // lanes
    stride = spread_ref.shape[0] // tiles
    bags = out_ref.shape[0]
    factors = [
        spread_ref[pl.ds(i * stride, bags), :].astype(jnp.bfloat16) for i in range(tiles)
    ]
    out_ref[...] = jnp.dot(
        jnp.concatenate(factors, 1), table_ref[...], preferred_element_type=jnp.float32
    )

    for o in range(len(inexact)):

        @pl.when(jnp.max(inexact[o]) > 0)
        def _(o=o):
            factors = jnp.concatenate(
                [spread_ref[pl.ds((8 * o + i) * stride, bags), :] for i in range(8)], 1
            )
            rest = factors - factors.astype(jnp.bfloat16).astype(jnp.float32)
            out_ref[...] += jnp.dot(
                rest.astype(jnp.bfloat16),
                table_ref[pl.ds(8 * o * lanes, 8 * lanes), :],
                preferred_element_type=jnp.float32,
            )


def exact_so_far(tiles):
    return tuple(jnp.zeros((8, lanes), jnp.float32) for _ in range(tiles // 8))


def send_kernel(
    start_ref,
    core_ref,
    index_ref,
    weight_ref,
    length_ref,
    table_hbm,
    out_ref,
    high_ref,
    low_ref,
    factor_ref,
    rounds_ref,
    table_ref,
    rank_ref,
    code_ref,
    high_later,
    low_later,
    factor_later,
    spread_ref,
    table_sem,
):
    table_copy = pltpu.make_async_copy(table_hbm, table_ref, table_sem)
    table_copy.start()
    rows = table_ref.shape[0]
    tiles = rows // lanes
    core = 1 - core_ref[0]
    rounds = read_positions(
        start_ref, index_ref, weight_ref, length_ref, rank_ref, code_ref, rows
    )
    rounds_ref[0] = rounds
    slot_refs = (high_ref, low_ref, factor_ref)
    later_refs = (high_later, low_later, factor_later)
    fill_slots(rank_ref, code_ref, slot_refs, jnp.int32(0))
    inexact = spread_half(slot_refs, spread_ref, core, tiles, exact_so_far(tiles), False)

    def later_round(number, inexact):
        fill_slots(rank_ref, code_ref, later_refs, number * slots)
        return spread_half(later_refs, spread_ref, core, tiles, inexact, True)

    inexact = lax.fori_loop(1, rounds, later_round, inexact)
    table_copy.wait()
    multiply(spread_ref, table_ref, inexact, out_ref)


def keep_kernel(
    start_ref,
    core_ref,
    rounds_ref,
    high_ref,
    low_ref,
    factor_ref,
    index_hbm,
    weight_hbm,
    length_hbm,
    table_hbm,
    out_ref,
    table_ref,
    index_ref,
    weight_ref,
    length_ref,
    rank_ref,
    code_ref,
    high_later,
    low_later,
    factor_later,
    spread_ref,
    table_sem,
    index_sem,
    weight_sem,
    length_sem,
):
    table_copy = pltpu.make_async_copy(table_hbm, table_ref, table_sem)
    table_copy.start()
    rows = table_ref.shape[0]
    tiles = rows // lanes
    core = core_ref[0]
    slot_refs = (high_ref, low_ref, factor_ref)
    later_refs = (high_later, low_later, factor_later)
    inexact = spread_half(slot_refs, spread_ref, core, tiles, exact_so_far(tiles), False)
    rounds = rounds_ref[0]

    @pl.when(rounds > 1)
    def _():
        copies = [
            pltpu.make_async_copy(index_hbm, index_ref, index_sem),
            pltpu.make_async_copy(weight_hbm, weight_ref, weight_sem),
            pltpu.make_async_copy(length_hbm, length_ref, length_sem),
        ]
        for copy in copies:
            copy.start()
        for copy in copies:
            copy.wait()
        read_positions(start_ref, index_ref, weight_ref, length_ref, rank_ref, code_ref, rows)

    def later_round(number, inexact):
        fill_slots(rank_ref, code_ref, later_refs, number * slots)
        return spread_half(later_refs, spread_ref, core, tiles, inexact, True)

    inexact = lax.fori_loop(1, rounds, later_round, inexact)
    table_copy.wait()
    multiply(spread_ref, table_ref, inexact, out_ref)


def kernels(table_rows, index_rows, weight, length, row_start, core):
    rows, width = table_rows.shape
    bag, batch = weight.shape
    padded = bag + 8 - bag % 8
    groups = batch * slots // lanes
    half = batch // 2
    tiles = rows // lanes
    smem = pl.BlockSpec(memory_space=pltpu.SMEM)
    vmem = pl.BlockSpec(memory_space=pltpu.VMEM)
    far = pl.BlockSpec(memory_space=pl.ANY)
    table_scratch = pltpu.VMEM((rows, width), table_rows.dtype)
    by_position = [pltpu.VMEM((padded, batch), jnp.float32)] * 2
    by_group = [pltpu.VMEM((groups, lanes), jnp.float32)] * 3
    spread = pltpu.VMEM(((half + 1) * tiles, lanes), jnp.float32)
    dma = pltpu.SemaphoreType.DMA
    pools = jax.ShapeDtypeStruct((half, width), jnp.float32)
    slot = jax.ShapeDtypeStruct((groups, lanes), jnp.float32)
    place = (row_start.reshape(1), core.reshape(1))

    sent, high, low, factor, rounds = pl.pallas_call(
        send_kernel,
        out_shape=(pools, slot, slot, slot, jax.ShapeDtypeStruct((1,), jnp.int32)),
        in_specs=[smem, smem, vmem, vmem, vmem, far],
        out_specs=(vmem, vmem, vmem, vmem, smem),
        scratch_shapes=[table_scratch, *by_position, *by_group, spread, dma],
    )(*place, index_rows, weight, length, table_rows)

    def keep():
        return pl.pallas_call(
            keep_kernel,
            out_shape=pools,
            in_specs=[smem, smem, smem, vmem, vmem, vmem, far, far, far, far],
            out_specs=vmem,
            scratch_shapes=[
                table_scratch,
                pltpu.VMEM(index_rows.shape, index_rows.dtype),
                pltpu.VMEM(weight.shape, weight.dtype),
                pltpu.VMEM(length.shape, length.dtype),
                *by_position,
                *by_group,
                spread,
                dma,
                dma,
                dma,
                dma,
            ],
            cost_estimate=pl.CostEstimate(
                flops=8 * half * rows * width, bytes_accessed=rows * width * 2, transcendentals=0
            ),
        )(*place, rounds, high, low, factor, index_rows, weight, length, table_rows)

    return sent, keep


def on_device(tables, indices, weights, lengths):
    _, row_dev, feature_width = tables.shape
    batch_size = indices.shape[2]
    table_count = lax.axis_size("table")
    pair_count = lax.axis_size("pair")
    core = lax.axis_index("core").astype(jnp.int32)
    row = lax.axis_index("pair").astype(jnp.int32) * 2 + core
    index_rows = indices.transpose(1, 0, 2)
    sent, keep = kernels(tables[0], index_rows, weights[0], lengths, row * row_dev, core)
    received = lax.ppermute(sent, "core", [(0, 1), (1, 0)])
    partial = keep() + received
    share = batch_size // (table_count * pair_count * 2)
    tiles = partial.reshape(table_count * pair_count, share, feature_width)
    arrived = lax.all_to_all(tiles, ("table", "pair"), split_axis=0, concat_axis=0, tiled=True)
    shares = arrived.reshape(table_count, pair_count, share, feature_width)
    return shares.sum(axis=1).astype(jnp.bfloat16)


def solution(mesh):
    tables, rows = mesh.devices.shape
    by_core = Mesh(mesh.devices.reshape(tables, rows // 2, 2), ("table", "pair", "core"))
    row = ("pair", "core")
    placed = (
        P("table", row, None),
        P("table", None, None),
        P("table", None, None),
        P("table", None),
    )
    return jax.shard_map(
        on_device,
        mesh=by_core,
        in_specs=placed,
        out_specs=P(None, ("table", *row), None),
        check_vma=False,
    )
```

time: 222 us -> 41.9 us (0.19)
  local copies, waits for them, and re-layouts: 159 us -> 0 us
  blocking collectives: 38.3 us -> 24.2 us
  Pallas kernels: 0 us -> 12.5 us
  other arithmetic: 13.3 us -> 1.54 us
  matrix products: 10.4 us -> 0 us
  starting transfers between devices: 0 us -> 3.29 us
    gather x10 -> x0, local copies, waits for them, and re-layouts: 156 us -> none  [add_block(): gathered = jnp.take(table_rows, index_block, axis=0)]
    all_to_all x2 -> x1, blocking collectives: 38.3 us -> 24.2 us  [on_device(): lax.all_to_all(tiles, ('table', 'pair'), split_axis=0, concat_axis=0, til...]
    pallas_call x0 -> x2, Pallas kernels: none -> 12.5 us  [the longest x1 6.37 us: kernels(): pl.pallas_call(send_kernel, out_shape=(pools, slot, slot, slot, jax.Shape...]
    select_n x11 -> x0, other arithmetic: 11.1 us -> none  [the longest x10 10 us: add_block(): gathered = jnp.take(table_rows, index_block, axis=0)]
    dot_general x10 -> x0, matrix products: 10.4 us -> none  [add_block(): jnp.einsum('lb,lbd->bd', factor_block, gathered, preferred_element_type=j...]
    ppermute x0 -> x1, starting transfers between devices: none -> 3.29 us  [on_device(): received = lax.ppermute(sent, 'core', [(0, 1), (1, 0)])]
  transfers between devices with their start and end apart: 0 -> 1, of which waited for: 0 -> 0; matrix products, arithmetic and copies ran while one was open for 0% -> 0% of each run, Pallas kernels for 0% -> 15%
where the time goes in v5:
time: 41.9 us; the launch traced here: 41.6 us
  blocking collectives  24.2 us (58%)
  Pallas kernels  12.5 us (30%)
  starting transfers between devices  3.29 us (8%)
  other arithmetic  1.54 us (4%)
    all_to_all x1, blocking collectives, on_device(): lax.all_to_all(tiles, ('table', 'pair'), split_axis=0, concat_axis=0, til...  24.2 us
    pallas_call x1, Pallas kernels, kernels(): pl.pallas_call(send_kernel, out_shape=(pools, slot, slot, slot, jax.Shape...  6.37 us
    pallas_call x1, Pallas kernels, keep(): pl.pallas_call(keep_kernel, out_shape=pools, in_specs=[smem, smem, smem,...  6.09 us
    ppermute x1, starting transfers between devices, on_device(): received = lax.ppermute(sent, 'core', [(0, 1), (1, 0)])  3.29 us
    add x1, other arithmetic, on_device(): partial = keep() + received  0.92 us
  transfers between devices with their start and end apart: 1, of which 0 were waited for; matrix products, arithmetic and copies ran while one was open for 0% of the time, Pallas kernels for 15%

profile of v5, /device:TPU:1, one launch (start us, length us, event | category | flops | bytes accessed | tf_op | source)
XLA Modules:
  0.0 41.6 jit_solution(12169221036356308513)
XLA Ops:
  0.0 6.4 %shard_map.46 = (f32[256,128]{1,0:T(8,128)}, f32[64,128]{1,0:T(8,128)}, f32[64,128]{1,0:T(8,128)}, f32[64,128]{1,0:T(8,128)}, s32[1]{0:T(128)}) custom-call(s32[1]{0:T(128)} %bitcast.start_ref, s32[1]{0:T(128)} %bitcast.1.core_ref, s32[100,1,512]{2,1,0:T(1,128)} %bitcast.11, bf16[100,512]{1,0:T(8,128)(2,1)} %bitcast.13, s32[1,512]{1,0:T(1,128)} %length_hbm.1, ...), custom_call_target="tpu_custom_call" | custom-call | tf_op jit(solution)/shard_map/pallas_call | solution.py:265
  6.4 3.3 %collective-permute-start = (f32[256,128]{1,0:T(8,128)}, f32[256,128]{1,0:T(8,128)S(1)}, u32[]{:S(2)}, u32[]{:S(2)}) collective-permute-start(f32[256,128]{1,0:T(8,128)} %get-tuple-element.14), channel_id=1, source_target_pairs={{0,1},{1,0},{2,3},{3,2},{4,5},{5,4},{6,7},{7,6},{8,9},{9,8},{10,11... | collective-permute-start | bytes 393224 | tf_op jit(solution)/shard_map/ppermute | solution.py:309
  9.7 6.1 %shard_map.47 = f32[256,128]{1,0:T(8,128)} custom-call(s32[1]{0:T(128)} %bitcast.start_ref, s32[1]{0:T(128)} %bitcast.1.core_ref, s32[1]{0:T(128)} %get-tuple-element.10.rounds_ref, f32[64,128]{1,0:T(8,128)} %get-tuple-element.11.high_ref, f32[64,128]{1,0:T(8,128)} %get-tuple-element.12.low_ref, f32[64,128]{1,0:T(8,128)} %get-tuple-element.13.factor_ref, ...), custom_call_target="tpu_custom_call" | custom-call | flops 2147483648 | bytes 2097152 | tf_op jit(solution)/shard_map/pallas_call | solution.py:274
  15.8 0.0 collective-permute-done
  15.8 0.9 %add.7 = f32[256,128]{1,0:T(8,128)S(1)} add(f32[256,128]{1,0:T(8,128)} %shard_map.47, f32[256,128]{1,0:T(8,128)S(1)} %collective-permute-done) | non-fusion elementwise | flops 32768 | bytes 393216 | tf_op jit(solution)/shard_map/add | solution.py:310
  16.7 24.2 %all_to_all.5 = f32[128,2,128]{2,1,0:T(2,128)S(1)} all-to-all(f32[128,2,128]{2,1,0:T(2,128)S(1)} %bitcast.10), channel_id=1, replica_groups=mesh['table'=4,'pair'=32,'core'=2] {'table','pair'}, dimensions={0} | all-to-all | bytes 262144 | tf_op jit(solution)/shard_map/all_to_all | solution.py:313
  40.9 0.6 %bitcast_reduce_fusion = bf16[4,2,128]{2,1,0:T(2,128)(2,1)} fusion(f32[128,2,128]{2,1,0:T(2,128)S(1)} %all_to_all.5), kind=kLoop, calls=%fused_computation | loop fusion | flops 31744 | bytes 133120 | tf_op jit(solution)/shard_map/reduce_sum | solution.py:315
Async XLA Ops:
  6.4 9.4 %collective-permute-start = (f32[256,128]{1,0:T(8,128)}, f32[256,128]{1,0:T(8,128)S(1)}, u32[]{:S(2)}, u32[]{:S(2)}) collective-permute-start(f32[256,128]{1,0:T(8,128)} %get-tuple-element.14), channel_id=1, source_target_pairs={{0,1},{1,0},{2,3},{3,2},{4,5},{5,4},{6,7},{7,6},{8,9},{9,8},{10,11... | collective-permute-start | bytes 393224 | tf_op jit(solution)/shard_map/ppermute | solution.py:309
